TPU v7x, 32 devices: a whole 2x2x4 slice. The times are simulated.
32 devices in a mesh: rep: 4 (over z), fsdp: 2 (over x), tp: 4 (over y, core).
Axes of the slice: x: 2, y: 2, z: 4, core: 2. Of those that a mesh axis runs over, the one named last changes fastest.
Arguments:
- gate_pre: bfloat16 [1024, 14848], P(('rep', 'fsdp'), 'tp'), may hold values from -6 to 6
- up_pre: bfloat16 [1024, 14848], P(('rep', 'fsdp'), 'tp'), may hold values from -30 to 30
- out_grad: bfloat16 [1024, 4096], P(('rep', 'fsdp')), may hold values from -30 to 30
Outputs:
- down_grad: bfloat16 [4096, 14848], P('fsdp', 'tp')
All inputs are finite; a program needn't handle non-finite values.
Results may differ from a plain program's by a relative error of at most 0.02.
Values may be sent and summed in bfloat16 or wider, within the bound.
A program may use at most 128 MiB of HBM per device.

v0:
```python
import jax
import jax.numpy as jnp
from jax import lax
from jax.sharding import PartitionSpec as P


def on_device(gate_pre, up_pre, out_grad):
    hidden = (jax.nn.silu(gate_pre.astype(jnp.float32)) * up_pre.astype(jnp.float32)).astype(
        jnp.bfloat16
    )
    spread = lax.all_to_all(out_grad, "fsdp", split_axis=1, concat_axis=0, tiled=True)
    grad_rows = lax.all_gather(spread, "rep", axis=0, tiled=True)
    hidden_rows = lax.all_gather(hidden, ("rep", "fsdp"), axis=0, tiled=True)
    summed = lax.dot_general(
        grad_rows, hidden_rows, (((0,), (0,)), ((), ())), preferred_element_type=jnp.float32
    )
    square_total = lax.psum(jnp.sum(summed * summed), ("fsdp", "tp"))
    entry_count = summed.shape[0] * lax.axis_size("fsdp") * summed.shape[1] * lax.axis_size("tp")
    factor = 1.0 / jnp.sqrt(square_total / entry_count + 1e-06)
    return (summed * factor).astype(jnp.bfloat16)


def solution(mesh):
    return jax.shard_map(
        on_device,
        mesh=mesh,
        in_specs=(P(("rep", "fsdp"), "tp"), P(("rep", "fsdp"), "tp"), P(("rep", "fsdp"), None)),
        out_specs=P("fsdp", "tp"),
        check_vma=False,
    )
```

profile of v0, /device:TPU:0, one launch (start us, length us, event | category | flops | bytes accessed | tf_op | source)
XLA Modules:
  0.0 307.9 jit_solution(16072461343263493116)
XLA Ops:
  6.5 0.0 copy-start
  6.5 0.0 all-gather.5.cloned.1.call-start
  6.5 1.7 copy.6
  8.2 17.6 %all_to_all.19 = bf16[128,2,2048]{0,2,1:T(8,128)(2,1)S(1)} all-to-all(bf16[128,2,2048]{0,2,1:T(8,128)(2,1)S(1)} %bitcast.9), channel_id=1, replica_groups=mesh['rep'=4,'fsdp'=2,'tp'=4] {'fsdp'}, dimensions={1} | all-to-all | bytes 2097152 | tf_op jit(solution)/shard_map/all_to_all | solution.py:11
  25.9 1.3 copy.7
  27.2 0.0 all-gather.5.cloned.1.call-update
  27.2 0.0 all-gather.3.cloned.1.call-start
  27.2 0.0 copy-done
  27.3 2.7 fusion.5
  30.0 0.0 all-gather.3.cloned.1.call-update
  30.0 78.6 %all-gather.5.cloned.1.call-done = bf16[1024,2048]{1,0:T(8,128)(2,1)} async-done(((bf16[256,2048]{1,0:T(8,128)(2,1)}), bf16[1024,2048]{1,0:T(8,128)(2,1)}) %all-gather.5.cloned.1.call-update) | async-done | bytes 4194320 | tf_op jit(solution)/shard_map/all_gather | solution.py:12
  108.6 115.4 %all-gather.3.cloned.1.call-done = bf16[1024,3712]{1,0:T(8,128)(2,1)} async-done(((bf16[128,3712]{1,0:T(8,128)(2,1)}), bf16[1024,3712]{1,0:T(8,128)(2,1)}) %all-gather.3.cloned.1.call-update) | async-done | bytes 7602192 | tf_op jit(solution)/shard_map/all_gather | solution.py:13
  224.0 28.3 %multiply_reduce_fusion = (f32[]{:T(128)}, f32[3712,2048]{1,0:T(8,128)}) fusion(bf16[1024,3712]{1,0:T(8,128)(2,1)} %all-gather.3.cloned.1.call-done, bf16[1024,2048]{1,0:T(8,128)(2,1)} %all-gather.5.cloned.1.call-done), kind=kOutput, calls=%fused_computation.1 | convolution fusion | flops 15584460800 | bytes 42205188 | tf_op jit(solution)/shard_map/dot_general | solution.py:14
  252.3 12.4 %psum.7 = f32[]{:T(128)} all-reduce(f32[]{:T(128)} %get-tuple-element.5), channel_id=1, replica_groups=mesh['rep'=4,'fsdp'=2,'tp'=4] {'fsdp','tp'}, use_global_device_ids=true, to_apply=%region_1.2 | all-reduce | flops 1 | bytes 8 | tf_op jit(solution)/shard_map/psum | solution.py:17
  265.4 16.7 %fusion = bf16[2048,3712]{0,1:T(8,128)(2,1)} fusion(f32[3712,2048]{1,0:T(8,128)} %get-tuple-element.6, f32[]{:T(128)S(6)} %sqrt.3), kind=kLoop, calls=%fused_computation.2 | loop fusion | flops 15204352 | bytes 45613060 | tf_op jit(solution)/shard_map/convert_element_type | solution.py:20
  282.1 19.0 %copy.8 = bf16[2048,3712]{1,0:T(8,128)(2,1)} copy(bf16[2048,3712]{0,1:T(8,128)(2,1)} %fusion) | data formatting | bytes 30408704 | tf_op jit(solution)/shard_map/convert_element_type | solution.py:20
Async XLA Ops:
  6.5 20.7 %copy-start = (bf16[128,3712]{1,0:T(8,128)(2,1)S(1)}, bf16[128,3712]{1,0:T(8,128)(2,1)}, u32[]{:S(2)}) copy-start(bf16[128,3712]{1,0:T(8,128)(2,1)} %param.4) | copy-start | bytes 2850820
  6.5 102.1 %all-gather.5.cloned.1.call-start = ((), (), s32[]{:S(2)}) async-start(), calls=%async_computation.2 | async-start | bytes 5242880 | tf_op jit(solution)/shard_map/all_gather | solution.py:12
  27.2 196.8 %all-gather.3.cloned.1.call-start = ((), (), s32[]{:S(2)}) async-start(), calls=%async_computation.1 | async-start | bytes 8552448 | tf_op jit(solution)/shard_map/all_gather | solution.py:13
Sparse Core Ops, SparseCore 0:
  27.3 81.2 all-gather.4
  110.8 113.1 all-gather.2
where the time goes:
time: 309 us; the launch traced here: 308 us
  waiting for transfers between devices  194 us (63%)
  blocking collectives  30.1 us (10%)
  matrix products  28.3 us (9%)
  local copies, waits for them, and re-layouts  22 us (7%)
  other arithmetic  19.4 us (6%)
  between operations  14.1 us (5%)
    all_gather x1, waiting for transfers between devices, on_device(): hidden_rows = lax.all_gather(hidden, ('rep', 'fsdp'), axis=0, tiled=True)  115 us
    all_gather x1, waiting for transfers between devices, on_device(): grad_rows = lax.all_gather(spread, 'rep', axis=0, tiled=True)  78.6 us
    dot_general x1, matrix products, on_device(): lax.dot_general(grad_rows, hidden_rows, (((0,), (0,)), ((), ())), preferr...  28.3 us
    convert_element_type x1, local copies, waits for them, and re-layouts, on_device(): return (summed * factor).astype(jnp.bfloat16)  19 us
    all_to_all x1, blocking collectives, on_device(): lax.all_to_all(out_grad, 'fsdp', split_axis=1, concat_axis=0, tiled=True)  17.6 us
    convert_element_type x1, other arithmetic, on_device(): return (summed * factor).astype(jnp.bfloat16)  16.7 us
    psum x1, blocking collectives, on_device(): square_total = lax.psum(jnp.sum(summed * summed), ('fsdp', 'tp'))  12.4 us
  transfers between devices with their start and end apart: 2, of which 2 were waited for; matrix products, arithmetic and copies ran while one was open for 1% of the time, Pallas kernels for 0%

commit v1 on v0

--- a/solution.py
+++ b/solution.py
@@ -8,7 +8,10 @@
     hidden = (jax.nn.silu(gate_pre.astype(jnp.float32)) * up_pre.astype(jnp.float32)).astype(
         jnp.bfloat16
     )
-    spread = lax.all_to_all(out_grad, "fsdp", split_axis=1, concat_axis=0, tiled=True)
+    spread = jnp.concatenate(
+        lax.all_to_all(jnp.stack(jnp.split(out_grad, lax.axis_size("fsdp"), axis=1)), "fsdp", 0, 0),
+        axis=0,
+    )
     grad_rows = lax.all_gather(spread, "rep", axis=0, tiled=True)
     hidden_rows = lax.all_gather(hidden, ("rep", "fsdp"), axis=0, tiled=True)
     summed = lax.dot_general(

time: 309 us -> 287 us (0.929)
  local copies, waits for them, and re-layouts: 22 us -> 1.41 us
    convert_element_type x1 -> x0, local copies, waits for them, and re-layouts: 19 us -> none  [on_device(): return (summed * factor).astype(jnp.bfloat16)]
where the time goes in v1:
time: 287 us
  waiting for transfers between devices  195 us (68%)
  blocking collectives  30.8 us (11%)
  matrix products  27.6 us (10%)
  other arithmetic  17.6 us (6%)
  between operations  14.1 us (5%)
    all_gather x1, waiting for transfers between devices, on_device(): hidden_rows = lax.all_gather(hidden, ('rep', 'fsdp'), axis=0, tiled=True)  115 us
    all_gather x1, waiting for transfers between devices, on_device(): grad_rows = lax.all_gather(spread, 'rep', axis=0, tiled=True)  79.9 us
    dot_general x1, matrix products, on_device(): lax.dot_general(grad_rows, hidden_rows, (((0,), (0,)), ((), ())), preferr...  27.6 us
    all_to_all x1, blocking collectives, on_device(): lax.all_to_all(jnp.stack(jnp.split(out_grad, lax.axis_size('fsdp'), axis=...  18.3 us
    convert_element_type x1, other arithmetic, on_device(): return (summed * factor).astype(jnp.bfloat16)  16 us
    psum x1, blocking collectives, on_device(): square_total = lax.psum(jnp.sum(summed * summed), ('fsdp', 'tp'))  12.4 us
  transfers between devices with their start and end apart: 2, of which 2 were waited for; matrix products, arithmetic and copies ran while one was open for 1% of the time, Pallas kernels for 0%

profile of v1, /device:TPU:0, one launch (start us, length us, event | category | flops | bytes accessed | tf_op | source)
XLA Modules:
  0.0 286.9 jit_solution(17649946681174013479)
XLA Ops:
  6.5 0.0 copy-start
  6.5 0.0 copy-start.1
  6.5 0.0 all-gather.3.cloned.1.call-start
  6.5 1.4 slice_bitcast_fusion.1
  7.9 0.1 pad_maximum_fusion
  8.1 18.3 %all_to_all.5 = bf16[2,128,2048]{2,1,0:T(8,128)(2,1)} all-to-all(bf16[2,128,2048]{2,1,0:T(8,128)(2,1)S(1)} %pad_maximum_fusion), channel_id=1, replica_groups=mesh['rep'=4,'fsdp'=2,'tp'=4] {'fsdp'}, dimensions={0} | all-to-all | bytes 2097152 | tf_op jit(solution)/shard_map/all_to_all | solution.py:12
  26.4 0.0 all-gather.3.cloned.1.call-update
  26.4 0.0 all-gather.5.cloned.1.call-start
  26.5 0.0 copy-done
  26.5 0.0 copy-done.1
  26.5 1.5 fusion.4
  28.0 0.0 all-gather.5.cloned.1.call-update
  28.0 79.9 %all-gather.3.cloned.1.call-done = bf16[1024,2048]{1,0:T(8,128)(2,1)} async-done(((bf16[256,2048]{1,0:T(8,128)(2,1)}), bf16[1024,2048]{1,0:T(8,128)(2,1)}) %all-gather.3.cloned.1.call-update) | async-done | bytes 4194320 | tf_op jit(solution)/shard_map/all_gather | solution.py:15
  107.9 115.4 %all-gather.5.cloned.1.call-done = bf16[1024,3712]{1,0:T(8,128)(2,1)} async-done(((bf16[128,3712]{1,0:T(8,128)(2,1)}), bf16[1024,3712]{1,0:T(8,128)(2,1)}) %all-gather.5.cloned.1.call-update) | async-done | bytes 7602192 | tf_op jit(solution)/shard_map/all_gather | solution.py:16
  223.3 27.6 %multiply_reduce_fusion = (f32[]{:T(128)}, f32[2048,3712]{1,0:T(8,128)}) fusion(bf16[1024,2048]{1,0:T(8,128)(2,1)} %all-gather.3.cloned.1.call-done, bf16[1024,3712]{1,0:T(8,128)(2,1)} %all-gather.5.cloned.1.call-done), kind=kOutput, calls=%fused_computation.1 | convolution fusion | flops 15584460800 | bytes 42205188 | tf_op jit(solution)/shard_map/dot_general | solution.py:17
  250.9 12.4 %psum.7 = f32[]{:T(128)} all-reduce(f32[]{:T(128)} %get-tuple-element.7), channel_id=1, replica_groups=mesh['rep'=4,'fsdp'=2,'tp'=4] {'fsdp','tp'}, use_global_device_ids=true, to_apply=%region_1.2 | all-reduce | flops 1 | bytes 8 | tf_op jit(solution)/shard_map/psum | solution.py:20
  264.0 16.0 %multiply_convert_fusion = bf16[2048,3712]{1,0:T(8,128)(2,1)} fusion(f32[2048,3712]{1,0:T(8,128)} %get-tuple-element.8, f32[]{:T(128)S(6)} %sqrt.3), kind=kLoop, calls=%fused_computation | loop fusion | flops 15204352 | bytes 45613060 | tf_op jit(solution)/shard_map/convert_element_type | solution.py:23
Async XLA Ops:
  6.5 19.9 %copy-start = (bf16[128,3712]{1,0:T(8,128)(2,1)S(1)}, bf16[128,3712]{1,0:T(8,128)(2,1)}, u32[]{:S(2)}) copy-start(bf16[128,3712]{1,0:T(8,128)(2,1)} %param.4) | copy-start | bytes 2850820
  6.5 19.9 %copy-start.1 = (bf16[128,3712]{1,0:T(8,128)(2,1)S(1)}, bf16[128,3712]{1,0:T(8,128)(2,1)}, u32[]{:S(2)}) copy-start(bf16[128,3712]{1,0:T(8,128)(2,1)} %param.3) | copy-start | bytes 2850820
  6.5 101.3 %all-gather.3.cloned.1.call-start = ((), (), s32[]{:S(2)}) async-start(), calls=%async_computation.1 | async-start | bytes 5242880 | tf_op jit(solution)/shard_map/all_gather | solution.py:15
  26.4 196.9 %all-gather.5.cloned.1.call-start = ((), (), s32[]{:S(2)}) async-start(), calls=%async_computation.2 | async-start | bytes 8552448 | tf_op jit(solution)/shard_map/all_gather | solution.py:16
Sparse Core Ops, SparseCore 0:
  26.5 81.2 all-gather.2
  110.1 113.1 all-gather.4

commit v2 on v0

--- a/solution.py
+++ b/solution.py
@@ -9,7 +9,12 @@
         jnp.bfloat16
     )
     spread = lax.all_to_all(out_grad, "fsdp", split_axis=1, concat_axis=0, tiled=True)
-    grad_rows = lax.all_gather(spread, "rep", axis=0, tiled=True)
+    ring = [spread]
+    for hop in range(3):
+        ring.append(lax.ppermute(ring[-1], "rep", [(dev, (dev + 1) % 4) for dev in range(4)]))
+    grad_rows = jnp.roll(
+        jnp.concatenate(ring[::-1], axis=0), (lax.axis_index("rep") + 1) * ring[0].shape[0], axis=0
+    )
     hidden_rows = lax.all_gather(hidden, ("rep", "fsdp"), axis=0, tiled=True)
     summed = lax.dot_general(
         grad_rows, hidden_rows, (((0,), (0,)), ((), ())), preferred_element_type=jnp.float32

time: 309 us -> 263 us (0.85)
  waiting for transfers between devices: 194 us -> 135 us
  starting transfers between devices: 0.04 us -> 17.6 us
  local copies, waits for them, and re-layouts: 22 us -> 13 us
  blocking collectives: 30.1 us -> 36.8 us
    ppermute x0 -> x3, waiting for transfers between devices: none -> 135 us  [on_device(): lax.ppermute(ring[-1], 'rep', [(dev, (dev + 1) % 4) for dev in range(4)])]
    all_gather x1, waiting for transfers between devices: 115 us -> 0.01 us  [on_device(): hidden_rows = lax.all_gather(hidden, ('rep', 'fsdp'), axis=0, tiled=True)]
    all_gather x1 -> x0, waiting for transfers between devices: 78.6 us -> none  [on_device(): grad_rows = lax.all_gather(spread, 'rep', axis=0, tiled=True)]
    convert_element_type x1 -> x0, local copies, waits for them, and re-layouts: 19 us -> none  [on_device(): return (summed * factor).astype(jnp.bfloat16)]
    ppermute x0 -> x3, starting transfers between devices: none -> 17.6 us  [on_device(): lax.ppermute(ring[-1], 'rep', [(dev, (dev + 1) % 4) for dev in range(4)])]
    unnamed x3 -> x8, local copies, waits for them, and re-layouts: 1.7 us -> 11.4 us
    all_to_all x1, blocking collectives: 17.6 us -> 24.4 us  [on_device(): lax.all_to_all(out_grad, 'fsdp', split_axis=1, concat_axis=0, tiled=True)]
  transfers between devices with their start and end apart: 2 -> 4, of which waited for: 2 -> 3; matrix products, arithmetic and copies ran while one was open for 1% -> 5% of each run, Pallas kernels for 0% -> 0%
where the time goes in v2:
time: 263 us
  waiting for transfers between devices  135 us (51%)
  blocking collectives  36.8 us (14%)
  matrix products  27.6 us (10%)
  other arithmetic  19.1 us (7%)
  starting transfers between devices  17.6 us (7%)
  between operations  14.1 us (5%)
  local copies, waits for them, and re-layouts  13 us (5%)
    ppermute x3, waiting for transfers between devices, on_device(): lax.ppermute(ring[-1], 'rep', [(dev, (dev + 1) % 4) for dev in range(4)])  135 us
    dot_general x1, matrix products, on_device(): lax.dot_general(grad_rows, hidden_rows, (((0,), (0,)), ((), ())), preferr...  27.6 us
    all_to_all x1, blocking collectives, on_device(): lax.all_to_all(out_grad, 'fsdp', split_axis=1, concat_axis=0, tiled=True)  24.4 us
    ppermute x3, starting transfers between devices, on_device(): lax.ppermute(ring[-1], 'rep', [(dev, (dev + 1) % 4) for dev in range(4)])  17.6 us
    convert_element_type x1, other arithmetic, on_device(): return (summed * factor).astype(jnp.bfloat16)  16 us
    psum x1, blocking collectives, on_device(): square_total = lax.psum(jnp.sum(summed * summed), ('fsdp', 'tp'))  12.4 us
    unnamed x8, local copies, waits for them, and re-layouts  11.4 us
  transfers between devices with their start and end apart: 4, of which 3 were waited for; matrix products, arithmetic and copies ran while one was open for 5% of the time, Pallas kernels for 0%

profile of v2, /device:TPU:0, one launch (start us, length us, event | category | flops | bytes accessed | tf_op | source)
XLA Modules:
  0.0 262.8 jit_solution(4408487592586069644)
XLA Ops:
  6.5 0.0 all-gather.2.cloned.1.call-start
  6.5 3.0 %fusion.6 = bf16[128,3712]{1,0:T(8,128)(2,1)} fusion(bf16[128,3712]{1,0:T(8,128)(2,1)} %param.4, bf16[128,3712]{1,0:T(8,128)(2,1)} %param.3), kind=kLoop, calls=%fused_computation.10 | loop fusion | flops 3801088 | bytes 2850816 | tf_op jit(solution)/shard_map/convert_element_type | solution.py:8
  9.6 0.0 all-gather.2.cloned.1.call-update
  9.6 1.6 copy.4
  11.2 24.4 %all_to_all.19 = bf16[128,2,2048]{0,2,1:T(8,128)(2,1)S(1)} all-to-all(bf16[128,2,2048]{0,2,1:T(8,128)(2,1)S(1)} %bitcast.8), channel_id=1, replica_groups=mesh['rep'=4,'fsdp'=2,'tp'=4] {'fsdp'}, dimensions={1} | all-to-all | bytes 2097152 | tf_op jit(solution)/shard_map/all_to_all | solution.py:11
  35.7 0.5 copy.5
  36.2 1.9 collective-permute-start
  38.1 40.7 %collective-permute-done = bf16[256,2048]{1,0:T(8,128)(2,1)S(1)} collective-permute-done((bf16[256,2048]{1,0:T(8,128)(2,1)S(1)}, bf16[256,2048]{1,0:T(8,128)(2,1)S(1)}, u32[]{:S(2)}, u32[]{:S(2)}) %collective-permute-start) | collective-permute-done | bytes 1048608 | tf_op jit(solution)/shard_map/ppermute | solution.py:14
  78.8 0.0 collective-permute-start.1
  78.8 49.1 %collective-permute-done.1 = bf16[256,2048]{1,0:T(8,128)(2,1)S(1)} collective-permute-done((bf16[256,2048]{1,0:T(8,128)(2,1)S(1)}, bf16[256,2048]{1,0:T(8,128)(2,1)S(1)}, u32[]{:S(2)}, u32[]{:S(2)}) %collective-permute-start.1) | collective-permute-done | bytes 1048608 | tf_op jit(solution)/shard_map/ppermute | solution.py:14
  127.9 15.7 %collective-permute-start.2 = (bf16[256,2048]{1,0:T(8,128)(2,1)S(1)}, bf16[256,2048]{1,0:T(8,128)(2,1)}, u32[]{:S(2)}, u32[]{:S(2)}) collective-permute-start(bf16[256,2048]{1,0:T(8,128)(2,1)S(1)} %collective-permute-done.1), channel_id=1, source_target_pairs={{0,8},{8,16},{16,24},{24,0},{1,9},{9,17},{17,25},{25,1},{2,10},{10... | collective-permute-start | bytes 3145736 | tf_op jit(solution)/shard_map/ppermute | solution.py:14
  143.6 44.7 %collective-permute-done.2 = bf16[256,2048]{1,0:T(8,128)(2,1)} collective-permute-done((bf16[256,2048]{1,0:T(8,128)(2,1)S(1)}, bf16[256,2048]{1,0:T(8,128)(2,1)}, u32[]{:S(2)}, u32[]{:S(2)}) %collective-permute-start.2) | collective-permute-done | bytes 1048608 | tf_op jit(solution)/shard_map/ppermute | solution.py:14
  188.3 2.3 constant_dynamic-update-slice_fusion.7
  190.6 1.0 constant_dynamic-update-slice_fusion.6
  191.7 1.0 constant_dynamic-update-slice_fusion.5
  192.7 1.0 constant_dynamic-update-slice_fusion.4
  193.8 2.3 constant_dynamic-update-slice_fusion.3
  196.1 1.0 constant_dynamic-update-slice_fusion.2
  197.1 1.0 constant_dynamic-update-slice_fusion.1
  198.1 1.0 constant_dynamic-update-slice_fusion
  199.2 0.0 all-gather.2.cloned.1.call-done
  199.2 27.6 %multiply_reduce_fusion = (f32[]{:T(128)}, f32[2048,3712]{1,0:T(8,128)}) fusion(bf16[1024,3712]{1,0:T(8,128)(2,1)} %all-gather.2.cloned.1.call-done, bf16[2048,2048]{1,0:T(8,128)(2,1)} %constant_dynamic-update-slice_fusion, s32[]{:T(128)S(6)} %select_n.14), kind=kOutput, calls=%fused_computation.1 | convolution fusion | flops 15584460800 | bytes 42205192 | tf_op jit(solution)/shard_map/dot_general | solution.py:19
  226.8 12.4 %psum.7 = f32[]{:T(128)} all-reduce(f32[]{:T(128)} %get-tuple-element.5), channel_id=1, replica_groups=mesh['rep'=4,'fsdp'=2,'tp'=4] {'fsdp','tp'}, use_global_device_ids=true, to_apply=%region_1.2 | all-reduce | flops 1 | bytes 8 | tf_op jit(solution)/shard_map/psum | solution.py:22
  239.9 16.0 %multiply_convert_fusion = bf16[2048,3712]{1,0:T(8,128)(2,1)} fusion(f32[2048,3712]{1,0:T(8,128)} %get-tuple-element.6, f32[]{:T(128)S(6)} %sqrt.3), kind=kLoop, calls=%fused_computation | loop fusion | flops 15204352 | bytes 45613060 | tf_op jit(solution)/shard_map/convert_element_type | solution.py:25
Async XLA Ops:
  6.5 192.6 %all-gather.2.cloned.1.call-start = ((), (), s32[]{:S(2)}) async-start(), calls=%async_computation.1 | async-start | bytes 8552448 | tf_op jit(solution)/shard_map/all_gather | solution.py:18
  36.2 42.6 %collective-permute-start = (bf16[256,2048]{1,0:T(8,128)(2,1)S(1)}, bf16[256,2048]{1,0:T(8,128)(2,1)S(1)}, u32[]{:S(2)}, u32[]{:S(2)}) collective-permute-start(bf16[256,2048]{1,0:T(8,128)(2,1)S(1)} %bitcast.4), channel_id=1, source_target_pairs={{0,8},{8,16},{16,24},{24,0},{1,9},{9,17},{17,25},{25,1},{2,10},{10... | collective-permute-start | bytes 3145736 | tf_op jit(solution)/shard_map/ppermute | solution.py:14
  78.8 49.1 %collective-permute-start.1 = (bf16[256,2048]{1,0:T(8,128)(2,1)S(1)}, bf16[256,2048]{1,0:T(8,128)(2,1)S(1)}, u32[]{:S(2)}, u32[]{:S(2)}) collective-permute-start(bf16[256,2048]{1,0:T(8,128)(2,1)S(1)} %collective-permute-done), channel_id=1, source_target_pairs={{0,8},{8,16},{16,24},{24,0},{1,9},{9,17},{17,25},{25,1},{2,10},{10... | collective-permute-start | bytes 3145736 | tf_op jit(solution)/shard_map/ppermute | solution.py:14
  127.9 60.4 %collective-permute-start.2 = (bf16[256,2048]{1,0:T(8,128)(2,1)S(1)}, bf16[256,2048]{1,0:T(8,128)(2,1)}, u32[]{:S(2)}, u32[]{:S(2)}) collective-permute-start(bf16[256,2048]{1,0:T(8,128)(2,1)S(1)} %collective-permute-done.1), channel_id=1, source_target_pairs={{0,8},{8,16},{16,24},{24,0},{1,9},{9,17},{17,25},{25,1},{2,10},{10... | collective-permute-start | bytes 3145736 | tf_op jit(solution)/shard_map/ppermute | solution.py:14
Sparse Core Ops, SparseCore 0:
  9.7 175.5 all-gather.1
